TPU v7x, 32 devices: a whole 2x2x4 slice. The times are simulated.
32 devices in a mesh: lon: 16 (over z, y, x), lat: 2 (over core).
Axes of the slice: x: 2, y: 2, z: 4, core: 2. Of those that a mesh axis runs over, the one named last changes fastest.
Arguments:
- u_vel: float32 [40, 128, 1024], P(None, 'lon', 'lat'), may hold values from -6 to 6
- v_vel: float32 [40, 128, 1024], P(None, 'lon', 'lat'), may hold values from -6 to 6
- thickness: float32 [40], replicated, may hold values from 0.5 to 2
- depth: float32 [128, 1024], P('lon', 'lat'), may hold values from 0.5 to 2
- sea_mask: int32 [128, 1024], P('lon', 'lat'), may hold values 0 or 1
- damping: float32 [128, 1024], P('lon', 'lat'), may hold values from 0.1 to 2
- eta_prev: float32 [128, 1024], P('lon', 'lat'), may hold values from -6 to 6
Outputs:
- surface: float32 [128, 1024], P('lon', 'lat')
- residual: float32 [128, 1024], P('lon', 'lat')
All inputs are finite; a program needn't handle non-finite values. No bound on the sum of `sea_mask` on one device may be relied on, other than what follows from the above.
Results may differ from a plain program's by a relative error of at most 0.0003.
Values sent between devices are 32-bit elements; how exact they have to be, the bound alone decides.
A program may use at most 64 MiB of HBM per device.

v0:
```python
import math

import jax
import jax.numpy as jnp
from jax import lax
from jax.sharding import PartitionSpec as P

LEVELS = 40
ITERS = 3


def extended_2(block, sides, width):
    for axis, dim in sides:
        count = lax.axis_size(axis)
        forward = [(i, i + 1) for i in range(count - 1)]
        forward.append((count - 1, 0))
        backward = [(target, source) for source, target in forward]
        low = lax.ppermute(
            lax.slice_in_dim(block, block.shape[dim] - width, None, axis=dim), axis, forward
        )
        high = lax.ppermute(lax.slice_in_dim(block, 0, width, axis=dim), axis, backward)
        block = jnp.concatenate([low, block, high], axis=dim)
    return block


def close_walls(extended, width):
    position = lax.axis_index("lat")
    count = lax.axis_size("lat")
    total = extended.shape[-1]
    column = lax.broadcasted_iota(jnp.int32, extended.shape, extended.ndim - 1)
    bottom = jnp.logical_and(position == 0, column < width)
    top = jnp.logical_and(position == count - 1, column >= total - width)
    keep = jnp.logical_not(jnp.logical_or(bottom, top)).astype(jnp.float32)
    return extended * keep


def column_sum(thickness, velocity):
    return jnp.einsum("k,kxy->xy", thickness, velocity, precision=lax.Precision.HIGHEST) * (
        1.0 / math.sqrt(LEVELS)
    )


def apply_padded(padded, diag, coef_east, coef_west, coef_north, coef_south):
    field = padded[1:-1, 1:-1]
    result = diag * field - coef_east * padded[2:, 1:-1] - coef_west * padded[:-2, 1:-1]
    return result - coef_north * padded[1:-1, 2:] - coef_south * padded[1:-1, :-2]


def operate(field, diag, coef_east, coef_west, coef_north, coef_south):
    padded = extended_2(field, (("lon", 0), ("lat", 1)), 1)
    return apply_padded(padded, diag, coef_east, coef_west, coef_north, coef_south)


def body(u_vel, v_vel, thickness, depth, sea_mask, damping, eta_prev):
    wet = sea_mask.astype(jnp.float32)
    width = 2
    surface_fields = [depth, wet, damping, eta_prev]
    stacked = jnp.stack(
        [column_sum(thickness, u_vel), column_sum(thickness, v_vel)] + surface_fields, axis=0
    )
    extended = extended_2(stacked, (("lon", 1), ("lat", 2)), width)
    extended = close_walls(extended, width)
    sum_east = extended[0]
    sum_north = extended[1]
    rest = extended[2:]
    depth_ext = rest[0]
    wet_ext = rest[1]
    wet_x = wet_ext[:-1, :] * wet_ext[1:, :]
    face_x = wet_x * 0.5 * (depth_ext[:-1, :] + depth_ext[1:, :])
    flux_x = wet_x * sum_east[:-1, :]
    wet_y = wet_ext[:, :-1] * wet_ext[:, 1:]
    face_y = wet_y * 0.5 * (depth_ext[:, :-1] + depth_ext[:, 1:])
    flux_y = wet_y * sum_north[:, :-1]
    coef_east, coef_west = (face_x[1:, 1:-1], face_x[:-1, 1:-1])
    coef_north, coef_south = (face_y[1:-1, 1:], face_y[1:-1, :-1])
    diverge = flux_x[1:, 1:-1] - flux_x[:-1, 1:-1] + flux_y[1:-1, 1:] - flux_y[1:-1, :-1]
    wet_mid = wet_ext[1:-1, 1:-1]
    damp_mid = rest[2][1:-1, 1:-1]
    rhs_mid = wet_mid * (damp_mid * rest[3][1:-1, 1:-1] - diverge)
    diag_mid = damp_mid + coef_east + coef_west + coef_north + coef_south
    precond_mid = rhs_mid / jnp.where(diag_mid > 0.0, diag_mid, 1.0)
    coef_east, coef_west = (coef_east[1:-1, 1:-1], coef_west[1:-1, 1:-1])
    coef_north, coef_south = (coef_north[1:-1, 1:-1], coef_south[1:-1, 1:-1])
    rhs = rhs_mid[1:-1, 1:-1]
    diag = diag_mid[1:-1, 1:-1]

    def sums(residual, precond, image):
        return lax.psum((jnp.sum(residual * precond), jnp.sum(image * precond)), ("lon", "lat"))

    surface = jnp.zeros_like(rhs)
    residual = rhs
    precond = precond_mid[1:-1, 1:-1]
    image = apply_padded(precond_mid, diag, coef_east, coef_west, coef_north, coef_south)
    gamma_now, delta_now = sums(residual, precond, image)
    step_size = gamma_now / delta_now
    direction, along_dir = (precond, image)
    for sweep in range(ITERS):
        surface = surface + step_size * direction
        residual = residual - step_size * along_dir
        if sweep + 1 < ITERS:
            precond = residual / diag
            image = operate(precond, diag, coef_east, coef_west, coef_north, coef_south)
            gamma_next, delta_now = sums(residual, precond, image)
            ratio_next = gamma_next / gamma_now
            step_size = gamma_next / (delta_now - ratio_next * gamma_next / step_size)
            direction = precond + ratio_next * direction
            along_dir = image + ratio_next * along_dir
            gamma_now = gamma_next
    return (surface, residual)


def solution(mesh):
    placed = (
        P(None, "lon", "lat"),
        P(None, "lon", "lat"),
        P(),
        P("lon", "lat"),
        P("lon", "lat"),
        P("lon", "lat"),
        P("lon", "lat"),
    )
    return jax.shard_map(
        body,
        mesh=mesh,
        in_specs=placed,
        out_specs=(P("lon", "lat"), P("lon", "lat")),
        check_vma=False,
    )
```

profile of v0, /device:TPU:0, one launch (start us, length us, event | category | flops | bytes accessed | tf_op | source)
XLA Modules:
  0.0 168.9 jit_solution(18303557818421487441)
XLA Ops:
  0.6 0.0 copy-start
  0.6 0.0 copy-start.6
  0.7 0.0 copy-start.1
  0.7 1.1 copy-done
  1.7 1.4 fusion.2
  3.2 0.0 copy-done.6
  3.2 0.0 copy-done.1
  3.2 0.8 fusion
  4.0 0.0 copy-start.2
  4.0 0.7 copy-done.2
  4.7 0.0 copy-start.3
  4.7 0.7 copy-done.3
  5.4 0.0 copy-start.4
  5.4 0.7 copy-done.4
  6.1 0.0 copy-start.5
  6.1 0.7 copy-done.5
  6.9 3.0 %collective-permute-start = (f32[6,2,512]{2,1,0:T(2,128)S(1)}, f32[6,2,512]{2,1,0:T(2,128)S(1)}, u32[]{:S(2)}, u32[]{:S(2)}) collective-permute-start(f32[6,2,512]{2,1,0:T(2,128)S(1)} %get-tuple-element.33), channel_id=1, source_target_pairs={{0,2},{2,4},{4,6},{6,8},{8,10},{10,12},{12,14},{14,16},{16,18},{18... | collective-permute-start | bytes 73736 | tf_op jit(solution)/shard_map/ppermute | solution.py:18
  9.9 4.1 %collective-permute-start.1 = (f32[6,2,512]{2,1,0:T(2,128)S(1)}, f32[6,2,512]{2,1,0:T(2,128)S(1)}, u32[]{:S(2)}, u32[]{:S(2)}) collective-permute-start(f32[6,2,512]{2,1,0:T(2,128)S(1)} %get-tuple-element.34), channel_id=1, source_target_pairs={{2,0},{4,2},{6,4},{8,6},{10,8},{12,10},{14,12},{16,14},{18,16},{20... | collective-permute-start | bytes 73736 | tf_op jit(solution)/shard_map/ppermute | solution.py:21
  14.0 1.7 %collective-permute-done = f32[6,2,512]{2,1,0:T(2,128)S(1)} collective-permute-done((f32[6,2,512]{2,1,0:T(2,128)S(1)}, f32[6,2,512]{2,1,0:T(2,128)S(1)}, u32[]{:S(2)}, u32[]{:S(2)}) %collective-permute-start) | collective-permute-done | bytes 24608 | tf_op jit(solution)/shard_map/ppermute | solution.py:18
  15.7 0.0 collective-permute-done.1
  15.7 0.1 pad_maximum_fusion.2
  15.8 0.1 collective-permute-start.2
  15.9 0.5 collective-permute-start.3
  16.4 0.7 collective-permute-done.2
  17.1 0.2 collective-permute-done.3
  17.3 0.2 maximum_select_fusion
  17.5 0.1 slice_multiply_fusion
  17.6 0.2 fusion.4
  17.8 0.7 multiply_reduce_fusion.4
  18.5 40.5 %all-reduce.2 = (f32[]{:T(128)}, f32[]{:T(128)}) all-reduce(f32[]{:T(128)} %get-tuple-element.3, f32[]{:T(128)} %get-tuple-element.2), channel_id=1, replica_groups=mesh['lon'=16,'lat'=2] {'lon','lat'}, use_global_device_ids=true, to_apply=%region_1.2 | all-reduce | flops 2 | bytes 16 | tf_op jit(solution)/shard_map/psum | solution.py:88
  60.3 0.1 slice_divide_fusion.1
  60.4 2.3 %collective-permute-start.5 = (f32[1,512]{1,0:T(1,128)S(1)}, f32[1,512]{1,0:T(1,128)S(1)}, u32[]{:S(2)}, u32[]{:S(2)}) collective-permute-start(f32[1,512]{1,0:T(1,128)S(1)} %get-tuple-element.43), channel_id=1, source_target_pairs={{0,2},{2,4},{4,6},{6,8},{8,10},{10,12},{12,14},{14,16},{16,18},{18... | collective-permute-start | bytes 6152 | tf_op jit(solution)/shard_map/ppermute | solution.py:18
  62.8 3.3 %collective-permute-start.4 = (f32[1,512]{1,0:T(1,128)S(1)}, f32[1,512]{1,0:T(1,128)S(1)}, u32[]{:S(2)}, u32[]{:S(2)}) collective-permute-start(f32[1,512]{1,0:T(1,128)S(1)} %get-tuple-element.44), channel_id=1, source_target_pairs={{2,0},{4,2},{6,4},{8,6},{10,8},{12,10},{14,12},{16,14},{18,16},{20... | collective-permute-start | bytes 6152 | tf_op jit(solution)/shard_map/ppermute | solution.py:21
  66.1 1.6 collective-permute-done.5
  67.7 0.0 collective-permute-done.4
  67.7 0.1 pad_maximum_fusion.24
  67.8 0.0 collective-permute-start.6
  67.8 0.5 collective-permute-start.7
  68.3 0.7 collective-permute-done.6
  68.9 0.2 collective-permute-done.7
  69.1 0.8 multiply_reduce_fusion.2
  69.9 40.3 %all-reduce.1 = (f32[]{:T(128)}, f32[]{:T(128)}) all-reduce(f32[]{:T(128)} %get-tuple-element.7, f32[]{:T(128)} %get-tuple-element.6), channel_id=1, replica_groups=mesh['lon'=16,'lat'=2] {'lon','lat'}, use_global_device_ids=true, to_apply=%region_5.6 | all-reduce | flops 2 | bytes 16 | tf_op jit(solution)/shard_map/psum | solution.py:88
  114.5 0.1 slice_divide_fusion
  114.6 2.3 %collective-permute-start.9 = (f32[1,512]{1,0:T(1,128)S(1)}, f32[1,512]{1,0:T(1,128)S(1)}, u32[]{:S(2)}, u32[]{:S(2)}) collective-permute-start(f32[1,512]{1,0:T(1,128)S(1)} %get-tuple-element.41), channel_id=1, source_target_pairs={{0,2},{2,4},{4,6},{6,8},{8,10},{10,12},{12,14},{14,16},{16,18},{18... | collective-permute-start | bytes 6152 | tf_op jit(solution)/shard_map/ppermute | solution.py:18
  117.0 3.3 %collective-permute-start.8 = (f32[1,512]{1,0:T(1,128)S(1)}, f32[1,512]{1,0:T(1,128)S(1)}, u32[]{:S(2)}, u32[]{:S(2)}) collective-permute-start(f32[1,512]{1,0:T(1,128)S(1)} %get-tuple-element.42), channel_id=1, source_target_pairs={{2,0},{4,2},{6,4},{8,6},{10,8},{12,10},{14,12},{16,14},{18,16},{20... | collective-permute-start | bytes 6152 | tf_op jit(solution)/shard_map/ppermute | solution.py:21
  120.3 1.6 collective-permute-done.9
  121.9 0.0 collective-permute-done.8
  121.9 0.1 pad_maximum_fusion.21
  121.9 0.0 collective-permute-start.10
  122.0 0.5 collective-permute-start.11
  122.5 0.7 collective-permute-done.10
  123.1 0.2 collective-permute-done.11
  123.3 0.7 multiply_reduce_fusion
  124.0 40.4 %all-reduce = (f32[]{:T(128)}, f32[]{:T(128)}) all-reduce(f32[]{:T(128)} %get-tuple-element.5, f32[]{:T(128)} %get-tuple-element.4), channel_id=1, replica_groups=mesh['lon'=16,'lat'=2] {'lon','lat'}, use_global_device_ids=true, to_apply=%region_9.10 | all-reduce | flops 2 | bytes 16 | tf_op jit(solution)/shard_map/psum | solution.py:88
  168.2 0.7 multiply_subtract_fusion
  (12 shorter events, 0.1 us)
Async XLA Ops:
  0.6 1.1 copy-start
  0.6 2.5 %copy-start.6 = (f32[40]{0:T(128)S(1)}, f32[40]{0:T(128)}, u32[]{:S(2)}) copy-start(f32[40]{0:T(128)} %param.9) | copy-start | bytes 484
  0.7 2.5 %copy-start.1 = (f32[40,8,512]{2,1,0:T(8,128)S(1)}, f32[40,8,512]{2,1,0:T(8,128)}, u32[]{:S(2)}) copy-start(f32[40,8,512]{2,1,0:T(8,128)} %param.8) | copy-start | bytes 1966084
  4.0 0.7 copy-start.2
  4.7 0.7 copy-start.3
  5.4 0.7 copy-start.4
  6.1 0.7 copy-start.5
  6.9 8.8 %collective-permute-start = (f32[6,2,512]{2,1,0:T(2,128)S(1)}, f32[6,2,512]{2,1,0:T(2,128)S(1)}, u32[]{:S(2)}, u32[]{:S(2)}) collective-permute-start(f32[6,2,512]{2,1,0:T(2,128)S(1)} %get-tuple-element.33), channel_id=1, source_target_pairs={{0,2},{2,4},{4,6},{6,8},{8,10},{10,12},{12,14},{14,16},{16,18},{18... | collective-permute-start | bytes 73736 | tf_op jit(solution)/shard_map/ppermute | solution.py:18
  9.9 5.8 %collective-permute-start.1 = (f32[6,2,512]{2,1,0:T(2,128)S(1)}, f32[6,2,512]{2,1,0:T(2,128)S(1)}, u32[]{:S(2)}, u32[]{:S(2)}) collective-permute-start(f32[6,2,512]{2,1,0:T(2,128)S(1)} %get-tuple-element.34), channel_id=1, source_target_pairs={{2,0},{4,2},{6,4},{8,6},{10,8},{12,10},{14,12},{16,14},{18,16},{20... | collective-permute-start | bytes 73736 | tf_op jit(solution)/shard_map/ppermute | solution.py:21
  15.8 1.3 collective-permute-start.2
  15.9 1.4 collective-permute-start.3
  60.4 7.2 %collective-permute-start.5 = (f32[1,512]{1,0:T(1,128)S(1)}, f32[1,512]{1,0:T(1,128)S(1)}, u32[]{:S(2)}, u32[]{:S(2)}) collective-permute-start(f32[1,512]{1,0:T(1,128)S(1)} %get-tuple-element.43), channel_id=1, source_target_pairs={{0,2},{2,4},{4,6},{6,8},{8,10},{10,12},{12,14},{14,16},{16,18},{18... | collective-permute-start | bytes 6152 | tf_op jit(solution)/shard_map/ppermute | solution.py:18
  62.8 4.9 %collective-permute-start.4 = (f32[1,512]{1,0:T(1,128)S(1)}, f32[1,512]{1,0:T(1,128)S(1)}, u32[]{:S(2)}, u32[]{:S(2)}) collective-permute-start(f32[1,512]{1,0:T(1,128)S(1)} %get-tuple-element.44), channel_id=1, source_target_pairs={{2,0},{4,2},{6,4},{8,6},{10,8},{12,10},{14,12},{16,14},{18,16},{20... | collective-permute-start | bytes 6152 | tf_op jit(solution)/shard_map/ppermute | solution.py:21
  67.8 1.2 collective-permute-start.6
  67.8 1.3 collective-permute-start.7
  114.6 7.2 %collective-permute-start.9 = (f32[1,512]{1,0:T(1,128)S(1)}, f32[1,512]{1,0:T(1,128)S(1)}, u32[]{:S(2)}, u32[]{:S(2)}) collective-permute-start(f32[1,512]{1,0:T(1,128)S(1)} %get-tuple-element.41), channel_id=1, source_target_pairs={{0,2},{2,4},{4,6},{6,8},{8,10},{10,12},{12,14},{14,16},{16,18},{18... | collective-permute-start | bytes 6152 | tf_op jit(solution)/shard_map/ppermute | solution.py:18
  117.0 4.9 %collective-permute-start.8 = (f32[1,512]{1,0:T(1,128)S(1)}, f32[1,512]{1,0:T(1,128)S(1)}, u32[]{:S(2)}, u32[]{:S(2)}) collective-permute-start(f32[1,512]{1,0:T(1,128)S(1)} %get-tuple-element.42), channel_id=1, source_target_pairs={{2,0},{4,2},{6,4},{8,6},{10,8},{12,10},{14,12},{16,14},{18,16},{20... | collective-permute-start | bytes 6152 | tf_op jit(solution)/shard_map/ppermute | solution.py:21
  121.9 1.2 collective-permute-start.10
  122.0 1.3 collective-permute-start.11
where the time goes:
time: 170 us; the launch traced here: 169 us
  blocking collectives  121 us (71%)
  starting transfers between devices  20 us (12%)
  between operations  10.3 us (6%)
  waiting for transfers between devices  7.39 us (4%)
  local copies, waits for them, and re-layouts  3.97 us (2%)
  other arithmetic  3.8 us (2%)
  matrix products  2.22 us (1%)
    psum x3, blocking collectives, sums(): lax.psum((jnp.sum(residual * precond), jnp.sum(image * precond)), ('lon',...  121 us
    ppermute x6, starting transfers between devices, extended_2(): lax.ppermute(lax.slice_in_dim(block, 0, width, axis=dim), axis, backward)  11.3 us
    ppermute x6, starting transfers between devices, extended_2(): lax.ppermute(lax.slice_in_dim(block, block.shape[dim] - width, None, axis...  8.74 us
    ppermute x6, waiting for transfers between devices, extended_2(): lax.ppermute(lax.slice_in_dim(block, block.shape[dim] - width, None, axis...  5.9 us
    unnamed x16, local copies, waits for them, and re-layouts  3.92 us
  transfers between devices with their start and end apart: 12, of which 9 were waited for; matrix products, arithmetic and copies ran while one was open for 0% of the time, Pallas kernels for 0%

commit v1 on v0

v1 whole, which is shorter than its diff:
```python
import functools
import math

import jax
import jax.numpy as jnp
from jax import lax
from jax.experimental import pallas as pl
from jax.experimental.pallas import tpu as pltpu
from jax.sharding import PartitionSpec as P

MESH = pl.DeviceIdType.MESH
HALO = 4
FIELDS = 5
LANES = 128
ROWS = 8


def scalars(nu):
    def form(c, shift):
        total = None
        for i, ci in enumerate(c):
            for j, cj in enumerate(c):
                if j < i:
                    continue
                term = ci * cj * nu[i + j + shift]
                term = term if i == j else term + term
                total = term if total is None else total + term
        return total

    def apply(c):
        out = list(c) + [None]
        for k, ck in enumerate(c):
            out[k + 1] = -ck if out[k + 1] is None else out[k + 1] - ck
        return out

    def axpy(a, x, y):
        out = []
        for k in range(max(len(x), len(y))):
            if k >= len(x):
                out.append(y[k])
            elif k >= len(y):
                out.append(a * x[k])
            else:
                out.append(y[k] + a * x[k])
        return out

    one = jnp.ones_like(nu[0])
    residual = [one]
    direction = [one]
    gamma = nu[0]
    step = gamma / (nu[0] - nu[1])
    surface = [step]
    residual = axpy(-step, apply(direction), residual)
    for _ in range(2):
        gamma_next = form(residual, 0)
        delta = gamma_next - form(residual, 1)
        ratio = gamma_next / gamma
        step = gamma_next / (delta - ratio * gamma_next / step)
        direction = axpy(ratio, direction, residual)
        surface = axpy(step, direction, surface)
        residual = axpy(-step, apply(direction), residual)
        gamma = gamma_next
    return surface, residual


def kernel(
    lon_n, lat_n, lon_axis, lat_axis,
    thick, u_hbm, v_hbm, depth_hbm, mask_hbm, damp_hbm, eta_hbm,
    surface_out, residual_out,
    u_buf, v_buf, depth_v, mask_v, damp_v, eta_v,
    send_lon, recv_lon, send_lat, recv_lat, recv_diag, row_send, row_recv,
    load_sem, halo_send, halo_recv, all_send, all_recv,
):
    levels, rows, cols = u_hbm.shape
    n = lon_n * lat_n
    lon = lax.axis_index(lon_axis)
    lat = lax.axis_index(lat_axis)
    me = lon * lat_n + lat

    def peer(k):
        flat = lax.rem(me + k, n)
        return (flat // lat_n, lax.rem(flat, lat_n))

    def each_peer(f):
        if n <= 64:
            for k in range(1, n):
                f(k)
        else:
            lax.fori_loop(1, n, lambda k, c: (f(k), c)[1], 0)

    loads = []
    for k, (src, dst) in enumerate((
        (u_hbm, u_buf), (v_hbm, v_buf), (depth_hbm, depth_v), (mask_hbm, mask_v), (damp_hbm, damp_v), (eta_hbm, eta_v)
    )):
        copy = pltpu.make_async_copy(src, dst, load_sem.at[k])
        copy.start()
        loads.append(copy)

    barrier = pltpu.get_barrier_semaphore()
    each_peer(lambda k: pl.semaphore_signal(barrier, inc=1, device_id=peer(k), device_id_type=MESH))

    for copy in loads[2:]:
        copy.wait()
    wet_own = mask_v[...].astype(jnp.float32)
    damp_own = damp_v[...]
    own = [depth_v[...] * wet_own, damp_own, damp_own * eta_v[...]]
    scale = 1.0 / math.sqrt(levels)
    for copy, buf in ((loads[0], u_buf), (loads[1], v_buf)):
        copy.wait()
        total = [None] * 4
        for k in range(levels):
            term = thick[k] * buf[k]
            total[k % 4] = term if total[k % 4] is None else total[k % 4] + term
        own.append(((total[0] + total[1]) + (total[2] + total[3])) * scale)

    for f in range(FIELDS):
        send_lon[0, f] = own[f][:HALO]
        send_lon[1, f] = own[f][rows - HALO:]
        send_lat[0, f] = own[f][:, :LANES]
        send_lat[1, f] = own[f][:, cols - LANES:]

    pl.semaphore_wait(barrier, n - 1)

    west = lax.rem(lon + lon_n - 1, lon_n)
    east = lax.rem(lon + 1, lon_n)

    def remote(src, dst, sem, target):
        return pltpu.make_async_remote_copy(
            src_ref=src, dst_ref=dst, send_sem=halo_send.at[sem], recv_sem=halo_recv.at[sem],
            device_id=target, device_id_type=MESH,
        )

    lon_copies = [remote(send_lon.at[h], recv_lon.at[h], h, (west if h == 0 else east, lat)) for h in (0, 1)]
    lat_copies = []
    for part in (0, 1):
        other = lat - 1 if part == 0 else lat + 1
        piece = pl.ds(0, LANES) if part == 0 else pl.ds(cols - LANES, LANES)
        group = [remote(send_lat.at[part], recv_lat.at[part], 2 + part, (lon, other))]
        for h in (0, 1):
            group.append(remote(
                send_lon.at[h, :, :, piece], recv_diag.at[h, part], 4 + 2 * part + h, (west if h == 0 else east, other)
            ))
        lat_copies.append(group)
    has_south = lat > 0
    has_north = lat < lat_n - 1
    sends = (has_south, has_north)
    gets = (has_north, has_south)

    for copy in lon_copies:
        copy.start()
    for part in (0, 1):
        @pl.when(sends[part])
        def _():
            for copy in lat_copies[part][1:]:
                copy.start()
            lat_copies[part][0].start()

        @pl.when(jnp.logical_not(gets[part]))
        def _():
            recv_lat[part] = jnp.zeros((FIELDS, rows, LANES), jnp.float32)
            recv_diag[0, part] = jnp.zeros((FIELDS, HALO, LANES), jnp.float32)
            recv_diag[1, part] = jnp.zeros((FIELDS, HALO, LANES), jnp.float32)

    for part in (0, 1):
        @pl.when(gets[part])
        def _():
            for copy in lat_copies[part]:
                copy.wait_recv()
    for copy in lon_copies:
        copy.wait_recv()

    lane = lax.broadcasted_iota(jnp.int32, (rows, LANES), 1)
    north_side = lane < LANES // 2

    def extended(f):
        sides = jnp.where(north_side, recv_lat[0, f], recv_lat[1, f])
        over = jnp.concatenate([recv_lon[0, f], recv_lon[1, f]], axis=0)
        corner_north = jnp.concatenate([recv_diag[0, 0, f], recv_diag[1, 0, f]], axis=0)
        corner_south = jnp.concatenate([recv_diag[0, 1, f], recv_diag[1, 1, f]], axis=0)
        corner = jnp.where(north_side, corner_north, corner_south)
        return jnp.concatenate(
            [jnp.concatenate([own[f], sides], axis=1), jnp.concatenate([over, corner], axis=1)], axis=0
        )

    high, wide = 2 * rows, cols + LANES

    def up(x, axis):
        return pltpu.roll(x, x.shape[axis] - 1, axis)

    def down(x, axis):
        return pltpu.roll(x, 1, axis)

    deep, damp, forced, sum_east, sum_north = [extended(f) for f in range(FIELDS)]
    wet = (deep > 0.0).astype(jnp.float32)
    damp = jnp.where(damp > 0.0, damp, 1.0)
    wet_x = wet * up(wet, 0)
    wet_y = wet * up(wet, 1)
    face_x = wet_x * 0.5 * (deep + up(deep, 0))
    face_y = wet_y * 0.5 * (deep + up(deep, 1))
    flux_x = wet_x * sum_east
    flux_y = wet_y * sum_north
    rhs = wet * (forced - (flux_x - down(flux_x, 0) + flux_y - down(flux_y, 1)))
    face_w, face_s = down(face_x, 0), down(face_y, 1)
    inverse = 1.0 / (damp + face_x + face_w + face_y + face_s)

    def off(p):
        return face_x * up(p, 0) + face_w * down(p, 0) + face_y * up(p, 1) + face_s * down(p, 1)

    p0 = rhs * inverse
    w1 = off(p0)
    p1 = w1 * inverse
    w2 = off(p1)
    p2 = w2 * inverse
    w3 = off(p2)
    w0, w1, w2, w3, p0, p1, p2 = [x[:rows, :cols] for x in (rhs, w1, w2, w3, p0, p1, p2)]

    lines = []
    for a, b in ((w0, p0), (w0, p1), (w1, p1), (w1, p2), (w2, p2), (w3, p2)):
        product = a * b
        folded = product[:, :LANES]
        for c in range(LANES, cols, LANES):
            folded = folded + product[:, c:c + LANES]
        lines.append(jnp.sum(folded, axis=0, keepdims=True))
    zero = jnp.zeros_like(lines[0])
    table = jnp.concatenate(lines + [zero] * (8 - len(lines)), axis=0)
    table = jnp.broadcast_to(jnp.sum(table, axis=1, keepdims=True), (8, LANES))
    pick = lax.broadcasted_iota(jnp.int32, (8, LANES), 1) == lax.broadcasted_iota(jnp.int32, (8, LANES), 0)
    row = jnp.sum(jnp.where(pick, table, 0.0), axis=0, keepdims=True)
    row_send[...] = row
    row_recv[me] = row

    def send_row(k):
        pltpu.make_async_remote_copy(
            src_ref=row_send, dst_ref=row_recv.at[me], send_sem=all_send, recv_sem=all_recv,
            device_id=peer(k), device_id_type=MESH,
        ).start()

    each_peer(send_row)

    for copy in lon_copies:
        copy.wait_send()
    for part in (0, 1):
        @pl.when(sends[part])
        def _():
            for copy in lat_copies[part]:
                copy.wait_send()

    others = row_recv.at[pl.ds(0, n - 1)]
    pltpu.make_async_copy(others, others, all_recv).wait()
    total = jnp.sum(row_recv[...], axis=0)
    nu = [jnp.broadcast_to(total[:, k:k + 1], (ROWS, LANES)) for k in range(6)]
    s, r = scalars(nu)
    for c in range(0, cols, LANES):
        part = slice(c, c + LANES)
        surface_out[:, part] = s[0] * p0[:, part] + s[1] * p1[:, part] + s[2] * p2[:, part]
        residual_out[:, part] = (r[0] * w0[:, part] + r[1] * w1[:, part]) + (r[2] * w2[:, part] + r[3] * w3[:, part])
    pltpu.make_async_copy(others, others, all_send).wait()


def solution(mesh):
    lon_n, lat_n = mesh.shape["lon"], mesh.shape["lat"]
    n = lon_n * lat_n

    def body(u_vel, v_vel, thickness, depth, sea_mask, damping, eta_prev):
        levels, rows, cols = u_vel.shape
        f32 = jnp.float32
        hbm = pl.BlockSpec(memory_space=pl.ANY)
        vmem = pl.BlockSpec(memory_space=pltpu.VMEM)
        shape = jax.ShapeDtypeStruct((rows, cols), f32)
        return pl.pallas_call(
            functools.partial(kernel, lon_n, lat_n, "lon", "lat"),
            out_shape=(shape, shape),
            in_specs=[pl.BlockSpec(memory_space=pltpu.SMEM)] + [hbm] * 6,
            out_specs=(vmem, vmem),
            scratch_shapes=[
                pltpu.VMEM((levels, rows, cols), f32),
                pltpu.VMEM((levels, rows, cols), f32),
                pltpu.VMEM((rows, cols), f32),
                pltpu.VMEM((rows, cols), jnp.int32),
                pltpu.VMEM((rows, cols), f32),
                pltpu.VMEM((rows, cols), f32),
                pltpu.VMEM((2, FIELDS, HALO, cols), f32),
                pltpu.VMEM((2, FIELDS, HALO, cols), f32),
                pltpu.VMEM((2, FIELDS, rows, LANES), f32),
                pltpu.VMEM((2, FIELDS, rows, LANES), f32),
                pltpu.VMEM((2, 2, FIELDS, HALO, LANES), f32),
                pltpu.VMEM((1, LANES), f32),
                pltpu.VMEM((n, 1, LANES), f32),
                pltpu.SemaphoreType.DMA((6,)),
                pltpu.SemaphoreType.DMA((8,)),
                pltpu.SemaphoreType.DMA((8,)),
                pltpu.SemaphoreType.DMA,
                pltpu.SemaphoreType.DMA,
            ],
            compiler_params=pltpu.CompilerParams(collective_id=0, has_side_effects=True),
        )(thickness, u_vel, v_vel, depth, sea_mask, damping, eta_prev)

    placed = P("lon", "lat")
    return jax.shard_map(
        body,
        mesh=mesh,
        in_specs=(P(None, "lon", "lat"), P(None, "lon", "lat"), P(), placed, placed, placed, placed),
        out_specs=(placed, placed),
        check_vma=False,
    )
```

time: 170 us -> 21.1 us (0.12)
  blocking collectives: 121 us -> 0 us
  starting transfers between devices: 20 us -> 0 us
  Pallas kernels: 0 us -> 18.3 us
  between operations: 10.3 us -> 0.65 us
  waiting for transfers between devices: 7.39 us -> 0 us
  other arithmetic: 3.8 us -> 0 us
  matrix products: 2.22 us -> 0 us
  local copies, waits for them, and re-layouts: 3.97 us -> 1.94 us
    psum x3 -> x0, blocking collectives: 121 us -> none  [sums(): lax.psum((jnp.sum(residual * precond), jnp.sum(image * precond)), ('lon',...]
    ppermute x12 -> x0, starting transfers between devices: 20 us -> none  [the longest x6 11.3 us: extended_2(): lax.ppermute(lax.slice_in_dim(block, 0, width, axis=dim), axis, backward)]
    pallas_call x0 -> x1, Pallas kernels: none -> 18.3 us  [body(): pl.pallas_call(functools.partial(kernel, lon_n, lat_n, 'lon', 'lat'), out...]
    ppermute x12 -> x0, waiting for transfers between devices: 7.39 us -> none  [the longest x6 5.9 us: extended_2(): lax.ppermute(lax.slice_in_dim(block, block.shape[dim] - width, None, axis...]
    dot_general x2 -> x0, matrix products: 2.22 us -> none  [column_sum(): jnp.einsum('k,kxy->xy', thickness, velocity, precision=lax.Precision.HIGH...]
    reduce_sum x3 -> x0, other arithmetic: 2.21 us -> none  [sums(): jnp.sum(image * precond)]
    unnamed x16 -> x4, local copies, waits for them, and re-layouts: 3.92 us -> 1.94 us
  transfers between devices with their start and end apart: 12 -> 0, of which waited for: 9 -> 0; matrix products, arithmetic and copies ran while one was open for 0% -> 0% of each run, Pallas kernels for 0% -> 0%
where the time goes in v1:
time: 21.1 us; the launch traced here: 20.9 us
  Pallas kernels  18.3 us (87%)
  local copies, waits for them, and re-layouts  1.94 us (9%)
  between operations  0.65 us (3%)
    pallas_call x1, Pallas kernels, body(): pl.pallas_call(functools.partial(kernel, lon_n, lat_n, 'lon', 'lat'), out...  18.3 us
    unnamed x4, local copies, waits for them, and re-layouts  1.94 us

profile of v1, /device:TPU:0, one launch (start us, length us, event | category | flops | bytes accessed | tf_op | source)
XLA Modules:
  0.0 20.9 jit_solution(5721591397953842078)
XLA Ops:
  0.6 18.3 %shard_map.86 = (f32[8,512]{1,0:T(8,128)}, f32[8,512]{1,0:T(8,128)}) custom-call(f32[40]{0:T(128)} %thick.1, f32[40,8,512]{2,1,0:T(8,128)} %u_hbm.1, f32[40,8,512]{2,1,0:T(8,128)} %v_hbm.1, f32[8,512]{1,0:T(8,128)} %depth_hbm.1, s32[8,512]{1,0:T(8,128)} %mask_hbm.1, f32[8,512]{1,0:T(8,128)} %damp_hbm.1, f32[8,512]{1,0:T(8,128)} %eta_hbm.1), custom_call_target="tpu_custom_call" | custom-call | tf_op jit(solution)/shard_map/pallas_call | solution.py:270
  18.9 0.0 copy-start
  19.0 1.3 %copy.11 = f32[8,512]{1,0:T(8,128)} copy(f32[8,512]{1,0:T(8,128)} %get-tuple-element.4) | data formatting | bytes 32768
  20.3 0.0 copy-done
  20.3 0.6 %copy.12 = f32[8,512]{1,0:T(8,128)} copy(f32[8,512]{1,0:T(8,128)S(1)} %copy-done) | data formatting | bytes 32768
Async XLA Ops:
  18.9 1.3 %copy-start = (f32[8,512]{1,0:T(8,128)S(1)}, f32[8,512]{1,0:T(8,128)}, u32[]{:S(2)}) copy-start(f32[8,512]{1,0:T(8,128)} %get-tuple-element.5) | copy-start | bytes 49156

commit v2 on v1

--- a/solution.py
+++ b/solution.py
@@ -65,9 +65,9 @@
 
 def kernel(
     lon_n, lat_n, lon_axis, lat_axis,
-    thick, u_hbm, v_hbm, depth_hbm, mask_hbm, damp_hbm, eta_hbm,
+    thick_hbm, u_hbm, v_hbm, depth_hbm, mask_hbm, damp_hbm, eta_hbm,
     surface_out, residual_out,
-    u_buf, v_buf, depth_v, mask_v, damp_v, eta_v,
+    thick, u_buf, v_buf, depth_v, mask_v, damp_v, eta_v,
     send_lon, recv_lon, send_lat, recv_lat, recv_diag, row_send, row_recv,
     load_sem, halo_send, halo_recv, all_send, all_recv,
 ):
@@ -83,14 +83,15 @@
 
     def each_peer(f):
         if n <= 64:
-            for k in range(1, n):
+            for k in sorted(range(1, n), key=lambda k: -min(k, n - k)):
                 f(k)
         else:
             lax.fori_loop(1, n, lambda k, c: (f(k), c)[1], 0)
 
     loads = []
     for k, (src, dst) in enumerate((
-        (u_hbm, u_buf), (v_hbm, v_buf), (depth_hbm, depth_v), (mask_hbm, mask_v), (damp_hbm, damp_v), (eta_hbm, eta_v)
+        (u_hbm, u_buf), (v_hbm, v_buf), (depth_hbm, depth_v), (mask_hbm, mask_v), (damp_hbm, damp_v), (eta_hbm, eta_v),
+        (thick_hbm, thick)
     )):
         copy = pltpu.make_async_copy(src, dst, load_sem.at[k])
         copy.start()
@@ -266,13 +267,14 @@
         f32 = jnp.float32
         hbm = pl.BlockSpec(memory_space=pl.ANY)
         vmem = pl.BlockSpec(memory_space=pltpu.VMEM)
-        shape = jax.ShapeDtypeStruct((rows, cols), f32)
+        shape = pltpu.VMEM((rows, cols), f32)
         return pl.pallas_call(
             functools.partial(kernel, lon_n, lat_n, "lon", "lat"),
             out_shape=(shape, shape),
-            in_specs=[pl.BlockSpec(memory_space=pltpu.SMEM)] + [hbm] * 6,
+            in_specs=[hbm] * 7,
             out_specs=(vmem, vmem),
             scratch_shapes=[
+                pltpu.SMEM((levels,), f32),
                 pltpu.VMEM((levels, rows, cols), f32),
                 pltpu.VMEM((levels, rows, cols), f32),
                 pltpu.VMEM((rows, cols), f32),
@@ -286,7 +288,7 @@
                 pltpu.VMEM((2, 2, FIELDS, HALO, LANES), f32),
                 pltpu.VMEM((1, LANES), f32),
                 pltpu.VMEM((n, 1, LANES), f32),
-                pltpu.SemaphoreType.DMA((6,)),
+                pltpu.SemaphoreType.DMA((7,)),
                 pltpu.SemaphoreType.DMA((8,)),
                 pltpu.SemaphoreType.DMA((8,)),
                 pltpu.SemaphoreType.DMA,

time: 21.1 us -> 19.5 us (0.924)
  Pallas kernels: 18.3 us -> 17.5 us
  local copies, waits for them, and re-layouts: 1.94 us -> 1.21 us
    pallas_call x1, Pallas kernels: 18.3 us -> 17.5 us  [body(): pl.pallas_call(functools.partial(kernel, lon_n, lat_n, 'lon', 'lat'), out...]
    unnamed x4 -> x2, local copies, waits for them, and re-layouts: 1.94 us -> 1.21 us
where the time goes in v2:
time: 19.5 us; the launch traced here: 19.4 us
  Pallas kernels  17.5 us (90%)
  local copies, waits for them, and re-layouts  1.21 us (6%)
  between operations  0.64 us (3%)
    pallas_call x1, Pallas kernels, body(): pl.pallas_call(functools.partial(kernel, lon_n, lat_n, 'lon', 'lat'), out...  17.5 us
    unnamed x2, local copies, waits for them, and re-layouts  1.21 us

profile of v2, /device:TPU:0, one launch (start us, length us, event | category | flops | bytes accessed | tf_op | source)
XLA Modules:
  0.0 19.4 jit_solution(5433988253524328876)
XLA Ops:
  0.6 17.5 %shard_map.86 = (f32[8,512]{1,0:T(8,128)S(1)}, f32[8,512]{1,0:T(8,128)S(1)}) custom-call(f32[40]{0:T(128)} %thick_hbm.1, f32[40,8,512]{2,1,0:T(8,128)} %u_hbm.1, f32[40,8,512]{2,1,0:T(8,128)} %v_hbm.1, f32[8,512]{1,0:T(8,128)} %depth_hbm.1, s32[8,512]{1,0:T(8,128)} %mask_hbm.1, f32[8,512]{1,0:T(8,128)} %damp_hbm.1, f32[8,512]{1,0:T(8,128)} %eta_hbm.1), custom_call_target="tpu_custom_call" | custom-call | tf_op jit(solution)/shard_map/pallas_call | solution.py:271
  18.2 0.6 %copy.11 = f32[8,512]{1,0:T(8,128)} copy(f32[8,512]{1,0:T(8,128)S(1)} %get-tuple-element.2) | data formatting | bytes 32768
  18.8 0.6 %copy.12 = f32[8,512]{1,0:T(8,128)} copy(f32[8,512]{1,0:T(8,128)S(1)} %get-tuple-element.3) | data formatting | bytes 32768

commit v3 on v2

--- a/solution.py
+++ b/solution.py
@@ -68,7 +68,7 @@
     thick_hbm, u_hbm, v_hbm, depth_hbm, mask_hbm, damp_hbm, eta_hbm,
     surface_out, residual_out,
     thick, u_buf, v_buf, depth_v, mask_v, damp_v, eta_v,
-    send_lon, recv_lon, send_lat, recv_lat, recv_diag, row_send, row_recv,
+    send_lon, recv_lon, send_lat, recv_lat, send_diag, recv_diag, row_send, row_recv,
     load_sem, halo_send, halo_recv, all_send, all_recv,
 ):
     levels, rows, cols = u_hbm.shape
@@ -100,23 +100,58 @@
     barrier = pltpu.get_barrier_semaphore()
     each_peer(lambda k: pl.semaphore_signal(barrier, inc=1, device_id=peer(k), device_id_type=MESH))
 
+    def up(x, axis):
+        return pltpu.roll(x, x.shape[axis] - 1, axis)
+
+    def down(x, axis):
+        return pltpu.roll(x, 1, axis)
+
     for copy in loads[2:]:
         copy.wait()
     wet_own = mask_v[...].astype(jnp.float32)
     damp_own = damp_v[...]
-    own = [depth_v[...] * wet_own, damp_own, damp_own * eta_v[...]]
+    deep_own = depth_v[...] * wet_own
+    forced_own = wet_own * (damp_own * eta_v[...])
+    row_own = lax.broadcasted_iota(jnp.int32, (rows, cols), 0)
+    col_own = lax.broadcasted_iota(jnp.int32, (rows, cols), 1)
+    inner_x = jnp.where(row_own < rows - 1, wet_own * up(wet_own, 0), 0.0)
+    inner_y = jnp.where(col_own < cols - 1, wet_own * up(wet_own, 1), 0.0)
     scale = 1.0 / math.sqrt(levels)
+    column = []
     for copy, buf in ((loads[0], u_buf), (loads[1], v_buf)):
         copy.wait()
         total = [None] * 4
         for k in range(levels):
             term = thick[k] * buf[k]
             total[k % 4] = term if total[k % 4] is None else total[k % 4] + term
-        own.append(((total[0] + total[1]) + (total[2] + total[3])) * scale)
-
+        column.append(((total[0] + total[1]) + (total[2] + total[3])) * scale)
+    east_own, north_own = column
+    inner_x = inner_x * east_own
+    inner_y = inner_y * north_own
+    part_own = forced_own - (inner_x - down(inner_x, 0) + inner_y - down(inner_y, 1))
+    last_east = jnp.broadcast_to(east_own[rows - 1:], (rows, cols))
+    part_sent = jnp.where(row_own == rows - HALO, last_east, part_own)
+    own = [deep_own, damp_own, part_own, east_own, north_own]
+    tiles = cols // LANES
+    lane_short = lax.broadcasted_iota(jnp.int32, (rows, LANES), 1)
+    for f, x in enumerate((deep_own, damp_own, part_sent)):
+        for c in range(tiles):
+            piece = x[:, c * LANES:(c + 1) * LANES]
+            send_lon[0, f * tiles + c] = piece[:HALO]
+            send_lon[1, f * tiles + c] = piece[rows - HALO:]
+    north_last = north_own[:, cols - LANES:]
+    send_lon[0, 3 * tiles] = north_last[:HALO]
+    send_lon[1, 3 * tiles] = north_last[rows - HALO:]
+    for part in (0, 1):
+        packed = None
+        for f, x in enumerate((deep_own, damp_own, part_sent, north_own)):
+            edge = x[:, :LANES] if part == 0 else x[:, cols - LANES:]
+            edge = edge if f == 0 else pltpu.roll(edge, HALO * f if part == 0 else LANES - HALO * f, 1)
+            away = lane_short if part == 0 else LANES - 1 - lane_short
+            packed = edge if packed is None else jnp.where(away >= HALO * f, edge, packed)
+        send_diag[0, part] = packed[:HALO]
+        send_diag[1, part] = packed[rows - HALO:]
     for f in range(FIELDS):
-        send_lon[0, f] = own[f][:HALO]
-        send_lon[1, f] = own[f][rows - HALO:]
         send_lat[0, f] = own[f][:, :LANES]
         send_lat[1, f] = own[f][:, cols - LANES:]
 
@@ -135,11 +170,10 @@
     lat_copies = []
     for part in (0, 1):
         other = lat - 1 if part == 0 else lat + 1
-        piece = pl.ds(0, LANES) if part == 0 else pl.ds(cols - LANES, LANES)
         group = [remote(send_lat.at[part], recv_lat.at[part], 2 + part, (lon, other))]
         for h in (0, 1):
             group.append(remote(
-                send_lon.at[h, :, :, piece], recv_diag.at[h, part], 4 + 2 * part + h, (west if h == 0 else east, other)
+                send_diag.at[h, part], recv_diag.at[h, part], 4 + 2 * part + h, (west if h == 0 else east, other)
             ))
         lat_copies.append(group)
     has_south = lat > 0
@@ -159,8 +193,8 @@
         @pl.when(jnp.logical_not(gets[part]))
         def _():
             recv_lat[part] = jnp.zeros((FIELDS, rows, LANES), jnp.float32)
-            recv_diag[0, part] = jnp.zeros((FIELDS, HALO, LANES), jnp.float32)
-            recv_diag[1, part] = jnp.zeros((FIELDS, HALO, LANES), jnp.float32)
+            recv_diag[0, part] = jnp.zeros((HALO, LANES), jnp.float32)
+            recv_diag[1, part] = jnp.zeros((HALO, LANES), jnp.float32)
 
     for part in (0, 1):
         @pl.when(gets[part])
@@ -170,37 +204,53 @@
     for copy in lon_copies:
         copy.wait_recv()
 
-    lane = lax.broadcasted_iota(jnp.int32, (rows, LANES), 1)
-    north_side = lane < LANES // 2
+    north_side = lane_short < LANES // 2
+    corners = [jnp.concatenate([recv_diag[0, part], recv_diag[1, part]], axis=0) for part in (0, 1)]
+
+    def side(f):
+        return jnp.where(north_side, recv_lat[0, f], recv_lat[1, f])
+
+    def corner(f):
+        north, south = corners
+        if f > 0:
+            north = pltpu.roll(north, LANES - HALO * f, 1)
+            south = pltpu.roll(south, HALO * f, 1)
+        return jnp.where(north_side, north, south)
+
+    def over(k):
+        return jnp.concatenate([recv_lon[0, k], recv_lon[1, k]], axis=0)
 
     def extended(f):
-        sides = jnp.where(north_side, recv_lat[0, f], recv_lat[1, f])
-        over = jnp.concatenate([recv_lon[0, f], recv_lon[1, f]], axis=0)
-        corner_north = jnp.concatenate([recv_diag[0, 0, f], recv_diag[1, 0, f]], axis=0)
-        corner_south = jnp.concatenate([recv_diag[0, 1, f], recv_diag[1, 1, f]], axis=0)
-        corner = jnp.where(north_side, corner_north, corner_south)
+        low = [over(f * tiles + c) for c in range(tiles)] + [corner(f)]
         return jnp.concatenate(
-            [jnp.concatenate([own[f], sides], axis=1), jnp.concatenate([over, corner], axis=1)], axis=0
+            [jnp.concatenate([own[f], side(f)], axis=1), jnp.concatenate(low, axis=1)], axis=0
         )
 
     high, wide = 2 * rows, cols + LANES
-
-    def up(x, axis):
-        return pltpu.roll(x, x.shape[axis] - 1, axis)
-
-    def down(x, axis):
-        return pltpu.roll(x, 1, axis)
-
-    deep, damp, forced, sum_east, sum_north = [extended(f) for f in range(FIELDS)]
+    row_ext = lax.broadcasted_iota(jnp.int32, (high, wide), 0)
+    col_ext = lax.broadcasted_iota(jnp.int32, (high, wide), 1)
+    deep, damp, part = [extended(f) for f in range(3)]
+    west_row = jnp.broadcast_to(part[high - HALO:high - HALO + 1], (rows, wide))
+    sum_east = jnp.concatenate([jnp.concatenate([own[3], side(3)], axis=1), west_row], axis=0)
+    strip = over(3 * tiles)
+    sum_north = jnp.concatenate(
+        [
+            jnp.concatenate([own[4], side(4)], axis=1),
+            jnp.concatenate([strip] * tiles + [corner(3)], axis=1),
+        ],
+        axis=0,
+    )
     wet = (deep > 0.0).astype(jnp.float32)
     damp = jnp.where(damp > 0.0, damp, 1.0)
     wet_x = wet * up(wet, 0)
     wet_y = wet * up(wet, 1)
     face_x = wet_x * 0.5 * (deep + up(deep, 0))
     face_y = wet_y * 0.5 * (deep + up(deep, 1))
-    flux_x = wet_x * sum_east
-    flux_y = wet_y * sum_north
-    rhs = wet * (forced - (flux_x - down(flux_x, 0) + flux_y - down(flux_y, 1)))
+    at_x = jnp.logical_or(row_ext == rows - 1, row_ext == high - 1)
+    at_y = jnp.logical_or(col_ext == cols - 1, col_ext == wide - 1)
+    flux_x = jnp.where(at_x, wet_x * sum_east, 0.0)
+    flux_y = jnp.where(at_y, wet_y * sum_north, 0.0)
+    rhs = part - (flux_x - down(flux_x, 0) + flux_y - down(flux_y, 1))
     face_w, face_s = down(face_x, 0), down(face_y, 1)
     inverse = 1.0 / (damp + face_x + face_w + face_y + face_s)
 
@@ -281,11 +331,12 @@
                 pltpu.VMEM((rows, cols), jnp.int32),
                 pltpu.VMEM((rows, cols), f32),
                 pltpu.VMEM((rows, cols), f32),
-                pltpu.VMEM((2, FIELDS, HALO, cols), f32),
-                pltpu.VMEM((2, FIELDS, HALO, cols), f32),
+                pltpu.VMEM((2, 3 * (cols // LANES) + 1, HALO, LANES), f32),
+                pltpu.VMEM((2, 3 * (cols // LANES) + 1, HALO, LANES), f32),
                 pltpu.VMEM((2, FIELDS, rows, LANES), f32),
                 pltpu.VMEM((2, FIELDS, rows, LANES), f32),
-                pltpu.VMEM((2, 2, FIELDS, HALO, LANES), f32),
+                pltpu.VMEM((2, 2, HALO, LANES), f32),
+                pltpu.VMEM((2, 2, HALO, LANES), f32),
                 pltpu.VMEM((1, LANES), f32),
                 pltpu.VMEM((n, 1, LANES), f32),
                 pltpu.SemaphoreType.DMA((7,)),

time: 19.5 us -> 19.4 us (level)
  no operation moved by 1% of the time
where the time goes in v3:
time: 19.4 us; the launch traced here: 19.2 us
  Pallas kernels  17.4 us (90%)
  local copies, waits for them, and re-layouts  1.21 us (6%)
  between operations  0.64 us (3%)
    pallas_call x1, Pallas kernels, body(): pl.pallas_call(functools.partial(kernel, lon_n, lat_n, 'lon', 'lat'), out...  17.4 us
    unnamed x2, local copies, waits for them, and re-layouts  1.21 us

profile of v3, /device:TPU:0, one launch (start us, length us, event | category | flops | bytes accessed | tf_op | source)
XLA Modules:
  0.0 19.2 jit_solution(10885319232830363941)
XLA Ops:
  0.6 17.4 %shard_map.86 = (f32[8,512]{1,0:T(8,128)S(1)}, f32[8,512]{1,0:T(8,128)S(1)}) custom-call(f32[40]{0:T(128)} %thick_hbm.1, f32[40,8,512]{2,1,0:T(8,128)} %u_hbm.1, f32[40,8,512]{2,1,0:T(8,128)} %v_hbm.1, f32[8,512]{1,0:T(8,128)} %depth_hbm.1, s32[8,512]{1,0:T(8,128)} %mask_hbm.1, f32[8,512]{1,0:T(8,128)} %damp_hbm.1, f32[8,512]{1,0:T(8,128)} %eta_hbm.1), custom_call_target="tpu_custom_call" | custom-call | tf_op jit(solution)/shard_map/pallas_call | solution.py:321
  18.0 0.6 %copy.11 = f32[8,512]{1,0:T(8,128)} copy(f32[8,512]{1,0:T(8,128)S(1)} %get-tuple-element.2) | data formatting | bytes 32768
  18.6 0.6 %copy.12 = f32[8,512]{1,0:T(8,128)} copy(f32[8,512]{1,0:T(8,128)S(1)} %get-tuple-element.3) | data formatting | bytes 32768

commit v4 on v3

--- a/solution.py
+++ b/solution.py
@@ -68,7 +68,8 @@
     thick_hbm, u_hbm, v_hbm, depth_hbm, mask_hbm, damp_hbm, eta_hbm,
     surface_out, residual_out,
     thick, u_buf, v_buf, depth_v, mask_v, damp_v, eta_v,
-    send_lon, recv_lon, send_lat, recv_lat, send_diag, recv_diag, row_send, row_recv,
+    send_east, recv_west, send_west, recv_east, send_lat, recv_lat,
+    send_diag_east, recv_diag_west, send_diag_west, recv_diag_east, row_send, row_recv,
     load_sem, halo_send, halo_recv, all_send, all_recv,
 ):
     levels, rows, cols = u_hbm.shape
@@ -130,27 +131,31 @@
     inner_y = inner_y * north_own
     part_own = forced_own - (inner_x - down(inner_x, 0) + inner_y - down(inner_y, 1))
     last_east = jnp.broadcast_to(east_own[rows - 1:], (rows, cols))
-    part_sent = jnp.where(row_own == rows - HALO, last_east, part_own)
+    part_sent = jnp.where(row_own == 0, last_east, part_own)
     own = [deep_own, damp_own, part_own, east_own, north_own]
     tiles = cols // LANES
     lane_short = lax.broadcasted_iota(jnp.int32, (rows, LANES), 1)
-    for f, x in enumerate((deep_own, damp_own, part_sent)):
+    for f, (x, y) in enumerate(((deep_own, deep_own), (damp_own, damp_own), (part_own, part_sent))):
         for c in range(tiles):
-            piece = x[:, c * LANES:(c + 1) * LANES]
-            send_lon[0, f * tiles + c] = piece[:HALO]
-            send_lon[1, f * tiles + c] = piece[rows - HALO:]
+            span = slice(c * LANES, (c + 1) * LANES)
+            send_west[f * tiles + c] = x[:HALO, span]
+            send_east[f * tiles + c] = y[:, span]
     north_last = north_own[:, cols - LANES:]
-    send_lon[0, 3 * tiles] = north_last[:HALO]
-    send_lon[1, 3 * tiles] = north_last[rows - HALO:]
-    for part in (0, 1):
+    send_west[3 * tiles] = north_last[:HALO]
+    send_east[3 * tiles] = north_last
+
+    def pack(fields, part):
         packed = None
-        for f, x in enumerate((deep_own, damp_own, part_sent, north_own)):
+        for f, x in enumerate(fields):
             edge = x[:, :LANES] if part == 0 else x[:, cols - LANES:]
             edge = edge if f == 0 else pltpu.roll(edge, HALO * f if part == 0 else LANES - HALO * f, 1)
             away = lane_short if part == 0 else LANES - 1 - lane_short
             packed = edge if packed is None else jnp.where(away >= HALO * f, edge, packed)
-        send_diag[0, part] = packed[:HALO]
-        send_diag[1, part] = packed[rows - HALO:]
+        return packed
+
+    for part in (0, 1):
+        send_diag_west[part] = pack((deep_own, damp_own, part_own, north_own), part)[:HALO]
+        send_diag_east[part] = pack((deep_own, damp_own, part_sent, north_own), part)
     for f in range(FIELDS):
         send_lat[0, f] = own[f][:, :LANES]
         send_lat[1, f] = own[f][:, cols - LANES:]
@@ -166,104 +171,109 @@
             device_id=target, device_id_type=MESH,
         )
 
-    lon_copies = [remote(send_lon.at[h], recv_lon.at[h], h, (west if h == 0 else east, lat)) for h in (0, 1)]
-    lat_copies = []
+    east_copy = remote(send_east, recv_west, 0, (east, lat))
+    west_copy = remote(send_west, recv_east, 1, (west, lat))
+    early, late = [], []
     for part in (0, 1):
         other = lat - 1 if part == 0 else lat + 1
-        group = [remote(send_lat.at[part], recv_lat.at[part], 2 + part, (lon, other))]
-        for h in (0, 1):
-            group.append(remote(
-                send_diag.at[h, part], recv_diag.at[h, part], 4 + 2 * part + h, (west if h == 0 else east, other)
-            ))
-        lat_copies.append(group)
+        early.append([
+            remote(send_diag_east.at[part], recv_diag_west.at[part], 2 + part, (east, other)),
+            remote(send_lat.at[part], recv_lat.at[part], 4 + part, (lon, other)),
+        ])
+        late.append(remote(send_diag_west.at[part], recv_diag_east.at[part], 6 + part, (west, other)))
     has_south = lat > 0
     has_north = lat < lat_n - 1
     sends = (has_south, has_north)
     gets = (has_north, has_south)
 
-    for copy in lon_copies:
-        copy.start()
+    east_copy.start()
     for part in (0, 1):
         @pl.when(sends[part])
         def _():
-            for copy in lat_copies[part][1:]:
+            for copy in early[part]:
                 copy.start()
-            lat_copies[part][0].start()
+
+    west_copy.start()
+    for part in (0, 1):
+        @pl.when(sends[part])
+        def _():
+            late[part].start()
 
         @pl.when(jnp.logical_not(gets[part]))
         def _():
             recv_lat[part] = jnp.zeros((FIELDS, rows, LANES), jnp.float32)
-            recv_diag[0, part] = jnp.zeros((HALO, LANES), jnp.float32)
-            recv_diag[1, part] = jnp.zeros((HALO, LANES), jnp.float32)
+            recv_diag_west[part] = jnp.zeros((rows, LANES), jnp.float32)
+            recv_diag_east[part] = jnp.zeros((HALO, LANES), jnp.float32)
 
     for part in (0, 1):
         @pl.when(gets[part])
         def _():
-            for copy in lat_copies[part]:
+            for copy in early[part]:
                 copy.wait_recv()
-    for copy in lon_copies:
-        copy.wait_recv()
+    east_copy.wait_recv()
 
     north_side = lane_short < LANES // 2
-    corners = [jnp.concatenate([recv_diag[0, part], recv_diag[1, part]], axis=0) for part in (0, 1)]
-
-    def side(f):
-        return jnp.where(north_side, recv_lat[0, f], recv_lat[1, f])
-
-    def corner(f):
-        north, south = corners
-        if f > 0:
-            north = pltpu.roll(north, LANES - HALO * f, 1)
-            south = pltpu.roll(south, HALO * f, 1)
-        return jnp.where(north_side, north, south)
-
-    def over(k):
-        return jnp.concatenate([recv_lon[0, k], recv_lon[1, k]], axis=0)
-
-    def extended(f):
-        low = [over(f * tiles + c) for c in range(tiles)] + [corner(f)]
-        return jnp.concatenate(
-            [jnp.concatenate([own[f], side(f)], axis=1), jnp.concatenate(low, axis=1)], axis=0
-        )
-
     high, wide = 2 * rows, cols + LANES
     row_ext = lax.broadcasted_iota(jnp.int32, (high, wide), 0)
     col_ext = lax.broadcasted_iota(jnp.int32, (high, wide), 1)
-    deep, damp, part = [extended(f) for f in range(3)]
-    west_row = jnp.broadcast_to(part[high - HALO:high - HALO + 1], (rows, wide))
-    sum_east = jnp.concatenate([jnp.concatenate([own[3], side(3)], axis=1), west_row], axis=0)
-    strip = over(3 * tiles)
-    sum_north = jnp.concatenate(
-        [
-            jnp.concatenate([own[4], side(4)], axis=1),
-            jnp.concatenate([strip] * tiles + [corner(3)], axis=1),
-        ],
-        axis=0,
+
+    def side(f):
+        return jnp.where(north_side, recv_lat[0, f], recv_lat[1, f])
+
+    tops = [jnp.concatenate([own[f], side(f)], axis=1) for f in range(FIELDS)]
+
+    def krylov(over, corners, last_row, at_x):
+        def corner(f):
+            north, south = corners
+            if f > 0:
+                north = pltpu.roll(north, LANES - HALO * f, 1)
+                south = pltpu.roll(south, HALO * f, 1)
+            return jnp.where(north_side, north, south)
+
+        def extended(f):
+            low = [over(f * tiles + c) for c in range(tiles)] + [corner(f)]
+            return jnp.concatenate([tops[f], jnp.concatenate(low, axis=1)], axis=0)
+
+        deep, damp, known = [extended(f) for f in range(3)]
+        sum_east = jnp.concatenate([tops[3], jnp.broadcast_to(last_row, (rows, wide))], axis=0)
+        low_north = jnp.concatenate([over(3 * tiles)] * tiles + [corner(3)], axis=1)
+        sum_north = jnp.concatenate([tops[4], low_north], axis=0)
+        wet = (deep > 0.0).astype(jnp.float32)
+        damp = jnp.where(damp > 0.0, damp, 1.0)
+        wet_x = wet * up(wet, 0)
+        wet_y = wet * up(wet, 1)
+        face_x = wet_x * 0.5 * (deep + up(deep, 0))
+        face_y = wet_y * 0.5 * (deep + up(deep, 1))
+        at_y = jnp.logical_or(col_ext == cols - 1, col_ext == wide - 1)
+        flux_x = jnp.where(at_x, wet_x * sum_east, 0.0)
+        flux_y = jnp.where(at_y, wet_y * sum_north, 0.0)
+        rhs = known - (flux_x - down(flux_x, 0) + flux_y - down(flux_y, 1))
+        face_w, face_s = down(face_x, 0), down(face_y, 1)
+        inverse = 1.0 / (damp + face_x + face_w + face_y + face_s)
+
+        def off(p):
+            return face_x * up(p, 0) + face_w * down(p, 0) + face_y * up(p, 1) + face_s * down(p, 1)
+
+        p0 = rhs * inverse
+        w1 = off(p0)
+        p1 = w1 * inverse
+        w2 = off(p1)
+        p2 = w2 * inverse
+        return rhs, w1, w2, off(p2), p0, p1, p2
+
+    corners_west = [recv_diag_west[part] for part in (0, 1)]
+    row_of_west = jnp.concatenate(
+        [recv_west[2 * tiles + c][:1] for c in range(tiles)]
+        + [jnp.where(
+            north_side,
+            pltpu.roll(corners_west[0], LANES - 2 * HALO, 1),
+            pltpu.roll(corners_west[1], 2 * HALO, 1),
+        )[:1]],
+        axis=1,
     )
-    wet = (deep > 0.0).astype(jnp.float32)
-    damp = jnp.where(damp > 0.0, damp, 1.0)
-    wet_x = wet * up(wet, 0)
-    wet_y = wet * up(wet, 1)
-    face_x = wet_x * 0.5 * (deep + up(deep, 0))
-    face_y = wet_y * 0.5 * (deep + up(deep, 1))
-    at_x = jnp.logical_or(row_ext == rows - 1, row_ext == high - 1)
-    at_y = jnp.logical_or(col_ext == cols - 1, col_ext == wide - 1)
-    flux_x = jnp.where(at_x, wet_x * sum_east, 0.0)
-    flux_y = jnp.where(at_y, wet_y * sum_north, 0.0)
-    rhs = part - (flux_x - down(flux_x, 0) + flux_y - down(flux_y, 1))
-    face_w, face_s = down(face_x, 0), down(face_y, 1)
-    inverse = 1.0 / (damp + face_x + face_w + face_y + face_s)
-
-    def off(p):
-        return face_x * up(p, 0) + face_w * down(p, 0) + face_y * up(p, 1) + face_s * down(p, 1)
-
-    p0 = rhs * inverse
-    w1 = off(p0)
-    p1 = w1 * inverse
-    w2 = off(p1)
-    p2 = w2 * inverse
-    w3 = off(p2)
-    w0, w1, w2, w3, p0, p1, p2 = [x[:rows, :cols] for x in (rhs, w1, w2, w3, p0, p1, p2)]
+    fields = krylov(lambda k: recv_west[k], corners_west, row_of_west, row_ext == high - 1)
+    upper = row_own < HALO
+    w0, w1, w2, w3, p0, p1, p2 = [jnp.where(upper, x[:rows, :cols], x[rows:, :cols]) for x in fields]
 
     lines = []
     for a, b in ((w0, p0), (w0, p1), (w1, p1), (w1, p2), (w2, p2), (w3, p2)):
@@ -288,13 +298,29 @@
 
     each_peer(send_row)
 
-    for copy in lon_copies:
-        copy.wait_send()
+    for part in (0, 1):
+        @pl.when(gets[part])
+        def _():
+            late[part].wait_recv()
+    west_copy.wait_recv()
+
+    corners = [
+        jnp.concatenate([recv_diag_east[part], recv_diag_west[part][rows - HALO:]], axis=0) for part in (0, 1)
+    ]
+    fields = krylov(
+        lambda k: jnp.concatenate([recv_east[k], recv_west[k][rows - HALO:]], axis=0),
+        corners, row_of_west, jnp.logical_or(row_ext == rows - 1, row_ext == high - 1),
+    )
+    w0, w1, w2, w3, p0, p1, p2 = [x[:rows, :cols] for x in fields]
+
+    east_copy.wait_send()
+    west_copy.wait_send()
     for part in (0, 1):
         @pl.when(sends[part])
         def _():
-            for copy in lat_copies[part]:
+            for copy in early[part]:
                 copy.wait_send()
+            late[part].wait_send()
 
     others = row_recv.at[pl.ds(0, n - 1)]
     pltpu.make_async_copy(others, others, all_recv).wait()
@@ -331,12 +357,16 @@
                 pltpu.VMEM((rows, cols), jnp.int32),
                 pltpu.VMEM((rows, cols), f32),
                 pltpu.VMEM((rows, cols), f32),
-                pltpu.VMEM((2, 3 * (cols // LANES) + 1, HALO, LANES), f32),
-                pltpu.VMEM((2, 3 * (cols // LANES) + 1, HALO, LANES), f32),
+                pltpu.VMEM((3 * (cols // LANES) + 1, rows, LANES), f32),
+                pltpu.VMEM((3 * (cols // LANES) + 1, rows, LANES), f32),
+                pltpu.VMEM((3 * (cols // LANES) + 1, HALO, LANES), f32),
+                pltpu.VMEM((3 * (cols // LANES) + 1, HALO, LANES), f32),
                 pltpu.VMEM((2, FIELDS, rows, LANES), f32),
                 pltpu.VMEM((2, FIELDS, rows, LANES), f32),
-                pltpu.VMEM((2, 2, HALO, LANES), f32),
-                pltpu.VMEM((2, 2, HALO, LANES), f32),
+                pltpu.VMEM((2, rows, LANES), f32),
+                pltpu.VMEM((2, rows, LANES), f32),
+                pltpu.VMEM((2, HALO, LANES), f32),
+                pltpu.VMEM((2, HALO, LANES), f32),
                 pltpu.VMEM((1, LANES), f32),
                 pltpu.VMEM((n, 1, LANES), f32),
                 pltpu.SemaphoreType.DMA((7,)),

time: 19.4 us -> 16.5 us (0.85)
  Pallas kernels: 17.4 us -> 14.5 us
    pallas_call x1, Pallas kernels: 17.4 us -> 14.5 us  [body(): pl.pallas_call(functools.partial(kernel, lon_n, lat_n, 'lon', 'lat'), out...]
where the time goes in v4:
time: 16.5 us; the launch traced here: 16.3 us
  Pallas kernels  14.5 us (88%)
  local copies, waits for them, and re-layouts  1.21 us (7%)
  between operations  0.64 us (4%)
    pallas_call x1, Pallas kernels, body(): pl.pallas_call(functools.partial(kernel, lon_n, lat_n, 'lon', 'lat'), out...  14.5 us
    unnamed x2, local copies, waits for them, and re-layouts  1.21 us

profile of v4, /device:TPU:0, one launch (start us, length us, event | category | flops | bytes accessed | tf_op | source)
XLA Modules:
  0.0 16.3 jit_solution(13277542975330651780)
XLA Ops:
  0.6 14.5 %shard_map.86 = (f32[8,512]{1,0:T(8,128)S(1)}, f32[8,512]{1,0:T(8,128)S(1)}) custom-call(f32[40]{0:T(128)} %thick_hbm.1, f32[40,8,512]{2,1,0:T(8,128)} %u_hbm.1, f32[40,8,512]{2,1,0:T(8,128)} %v_hbm.1, f32[8,512]{1,0:T(8,128)} %depth_hbm.1, s32[8,512]{1,0:T(8,128)} %mask_hbm.1, f32[8,512]{1,0:T(8,128)} %damp_hbm.1, f32[8,512]{1,0:T(8,128)} %eta_hbm.1), custom_call_target="tpu_custom_call" | custom-call | tf_op jit(solution)/shard_map/pallas_call | solution.py:347
  15.1 0.6 %copy.11 = f32[8,512]{1,0:T(8,128)} copy(f32[8,512]{1,0:T(8,128)S(1)} %get-tuple-element.2) | data formatting | bytes 32768
  15.7 0.6 %copy.12 = f32[8,512]{1,0:T(8,128)} copy(f32[8,512]{1,0:T(8,128)S(1)} %get-tuple-element.3) | data formatting | bytes 32768

commit v5 on v4

--- a/solution.py
+++ b/solution.py
@@ -66,7 +66,7 @@
 def kernel(
     lon_n, lat_n, lon_axis, lat_axis,
     thick_hbm, u_hbm, v_hbm, depth_hbm, mask_hbm, damp_hbm, eta_hbm,
-    surface_out, residual_out,
+    both_out,
     thick, u_buf, v_buf, depth_v, mask_v, damp_v, eta_v,
     send_east, recv_west, send_west, recv_east, send_lat, recv_lat,
     send_diag_east, recv_diag_west, send_diag_west, recv_diag_east, row_send, row_recv,
@@ -84,7 +84,7 @@
 
     def each_peer(f):
         if n <= 64:
-            for k in sorted(range(1, n), key=lambda k: -min(k, n - k)):
+            for k in sorted(range(1, n), key=lambda k: min(k, n - k)):
                 f(k)
         else:
             lax.fori_loop(1, n, lambda k, c: (f(k), c)[1], 0)
@@ -193,12 +193,7 @@
             for copy in early[part]:
                 copy.start()
 
-    west_copy.start()
-    for part in (0, 1):
-        @pl.when(sends[part])
-        def _():
-            late[part].start()
-
+    for part in (0, 1):
         @pl.when(jnp.logical_not(gets[part]))
         def _():
             recv_lat[part] = jnp.zeros((FIELDS, rows, LANES), jnp.float32)
@@ -221,6 +216,12 @@
         return jnp.where(north_side, recv_lat[0, f], recv_lat[1, f])
 
     tops = [jnp.concatenate([own[f], side(f)], axis=1) for f in range(FIELDS)]
+
+    west_copy.start()
+    for part in (0, 1):
+        @pl.when(sends[part])
+        def _():
+            late[part].start()
 
     def krylov(over, corners, last_row, at_x):
         def corner(f):
@@ -329,8 +330,8 @@
     s, r = scalars(nu)
     for c in range(0, cols, LANES):
         part = slice(c, c + LANES)
-        surface_out[:, part] = s[0] * p0[:, part] + s[1] * p1[:, part] + s[2] * p2[:, part]
-        residual_out[:, part] = (r[0] * w0[:, part] + r[1] * w1[:, part]) + (r[2] * w2[:, part] + r[3] * w3[:, part])
+        both_out[0, :, part] = s[0] * p0[:, part] + s[1] * p1[:, part] + s[2] * p2[:, part]
+        both_out[1, :, part] = (r[0] * w0[:, part] + r[1] * w1[:, part]) + (r[2] * w2[:, part] + r[3] * w3[:, part])
     pltpu.make_async_copy(others, others, all_send).wait()
 
 
@@ -343,12 +344,12 @@
         f32 = jnp.float32
         hbm = pl.BlockSpec(memory_space=pl.ANY)
         vmem = pl.BlockSpec(memory_space=pltpu.VMEM)
-        shape = pltpu.VMEM((rows, cols), f32)
-        return pl.pallas_call(
+        shape = pltpu.VMEM((2, rows, cols), f32)
+        both = pl.pallas_call(
             functools.partial(kernel, lon_n, lat_n, "lon", "lat"),
-            out_shape=(shape, shape),
+            out_shape=shape,
             in_specs=[hbm] * 7,
-            out_specs=(vmem, vmem),
+            out_specs=vmem,
             scratch_shapes=[
                 pltpu.SMEM((levels,), f32),
                 pltpu.VMEM((levels, rows, cols), f32),
@@ -377,6 +378,8 @@
             ],
             compiler_params=pltpu.CompilerParams(collective_id=0, has_side_effects=True),
         )(thickness, u_vel, v_vel, depth, sea_mask, damping, eta_prev)
+        return both[0], both[1]
+
 
     placed = P("lon", "lat")
     return jax.shard_map(

time: 16.5 us -> 15.5 us (0.939)
  local copies, waits for them, and re-layouts: 1.21 us -> 0.61 us
  Pallas kernels: 14.5 us -> 14.1 us
    unnamed x2 -> x0, local copies, waits for them, and re-layouts: 1.21 us -> none
    squeeze x0 -> x1, local copies, waits for them, and re-layouts: none -> 0.61 us  [body(): return (both[0], both[1])]
    pallas_call x1, Pallas kernels: 14.5 us -> 14.1 us  [body(): pl.pallas_call(functools.partial(kernel, lon_n, lat_n, 'lon', 'lat'), out...]
where the time goes in v5:
time: 15.5 us; the launch traced here: 15.4 us
  Pallas kernels  14.1 us (91%)
  between operations  0.64 us (4%)
  local copies, waits for them, and re-layouts  0.61 us (4%)
    pallas_call x1, Pallas kernels, body(): pl.pallas_call(functools.partial(kernel, lon_n, lat_n, 'lon', 'lat'), out...  14.1 us
    squeeze x1, local copies, waits for them, and re-layouts, body(): return (both[0], both[1])  0.61 us

profile of v5, /device:TPU:0, one launch (start us, length us, event | category | flops | bytes accessed | tf_op | source)
XLA Modules:
  0.0 15.4 jit_solution(2380411647297243917)
XLA Ops:
  0.6 14.1 %shard_map.86 = f32[2,8,512]{2,1,0:T(8,128)S(1)} custom-call(f32[40]{0:T(128)} %thick_hbm.1, f32[40,8,512]{2,1,0:T(8,128)} %u_hbm.1, f32[40,8,512]{2,1,0:T(8,128)} %v_hbm.1, f32[8,512]{1,0:T(8,128)} %depth_hbm.1, s32[8,512]{1,0:T(8,128)} %mask_hbm.1, f32[8,512]{1,0:T(8,128)} %damp_hbm.1, f32[8,512]{1,0:T(8,128)} %eta_hbm.1), custom_call_target="tpu_custom_call" | custom-call | tf_op jit(solution)/shard_map/pallas_call | solution.py:348
  14.8 0.6 %slice_bitcast_fusion = (f32[8,512]{1,0:T(8,128)}, f32[8,512]{1,0:T(8,128)}) fusion(f32[2,8,512]{2,1,0:T(8,128)S(1)} %shard_map.86), kind=kLoop, calls=%fused_computation | loop fusion | bytes 65536 | tf_op jit(solution)/shard_map/squeeze | solution.py:381

commit v6 on v5

--- a/solution.py
+++ b/solution.py
@@ -47,19 +47,23 @@
     one = jnp.ones_like(nu[0])
     residual = [one]
     direction = [one]
-    gamma = nu[0]
-    step = gamma / (nu[0] - nu[1])
+    under = nu[0] - nu[1]
+    step = nu[0] / under
+    inverse = 1.0 / nu[0]
+    step_inverse = under * inverse
     surface = [step]
     residual = axpy(-step, apply(direction), residual)
     for _ in range(2):
         gamma_next = form(residual, 0)
         delta = gamma_next - form(residual, 1)
-        ratio = gamma_next / gamma
-        step = gamma_next / (delta - ratio * gamma_next / step)
+        ratio = gamma_next * inverse
+        under = delta - ratio * gamma_next * step_inverse
+        step = gamma_next / under
+        inverse = 1.0 / gamma_next
+        step_inverse = under * inverse
         direction = axpy(ratio, direction, residual)
         surface = axpy(step, direction, surface)
         residual = axpy(-step, apply(direction), residual)
-        gamma = gamma_next
     return surface, residual
 
 
@@ -325,7 +329,13 @@
 
     others = row_recv.at[pl.ds(0, n - 1)]
     pltpu.make_async_copy(others, others, all_recv).wait()
-    total = jnp.sum(row_recv[...], axis=0)
+    if n <= 64:
+        heap = [row_recv[k] for k in range(n)]
+        while len(heap) > 1:
+            heap = [a + b for a, b in zip(heap[::2], heap[1::2])] + heap[len(heap) - len(heap) % 2:]
+        total = heap[0]
+    else:
+        total = jnp.sum(row_recv[...], axis=0)
     nu = [jnp.broadcast_to(total[:, k:k + 1], (ROWS, LANES)) for k in range(6)]
     s, r = scalars(nu)
     for c in range(0, cols, LANES):

time: 15.5 us -> 15.5 us (level)
  no operation moved by 1% of the time
where the time goes in v6:
time: 15.5 us; the launch traced here: 15.3 us
  Pallas kernels  14.1 us (91%)
  between operations  0.64 us (4%)
  local copies, waits for them, and re-layouts  0.61 us (4%)
    pallas_call x1, Pallas kernels, body(): pl.pallas_call(functools.partial(kernel, lon_n, lat_n, 'lon', 'lat'), out...  14.1 us
    squeeze x1, local copies, waits for them, and re-layouts, body(): return (both[0], both[1])  0.61 us

profile of v6, /device:TPU:0, one launch (start us, length us, event | category | flops | bytes accessed | tf_op | source)
XLA Modules:
  0.0 15.3 jit_solution(4475406227205655763)
XLA Ops:
  0.6 14.1 %shard_map.86 = f32[2,8,512]{2,1,0:T(8,128)S(1)} custom-call(f32[40]{0:T(128)} %thick_hbm.1, f32[40,8,512]{2,1,0:T(8,128)} %u_hbm.1, f32[40,8,512]{2,1,0:T(8,128)} %v_hbm.1, f32[8,512]{1,0:T(8,128)} %depth_hbm.1, s32[8,512]{1,0:T(8,128)} %mask_hbm.1, f32[8,512]{1,0:T(8,128)} %damp_hbm.1, f32[8,512]{1,0:T(8,128)} %eta_hbm.1), custom_call_target="tpu_custom_call" | custom-call | tf_op jit(solution)/shard_map/pallas_call | solution.py:358
  14.7 0.6 %slice_bitcast_fusion = (f32[8,512]{1,0:T(8,128)}, f32[8,512]{1,0:T(8,128)}) fusion(f32[2,8,512]{2,1,0:T(8,128)S(1)} %shard_map.86), kind=kLoop, calls=%fused_computation | loop fusion | bytes 65536 | tf_op jit(solution)/shard_map/squeeze | solution.py:391

commit v7 on v6

--- a/solution.py
+++ b/solution.py
@@ -99,8 +99,9 @@
         (thick_hbm, thick)
     )):
         copy = pltpu.make_async_copy(src, dst, load_sem.at[k])
+        loads.append(copy)
+    for copy in loads[2:] + loads[:2]:
         copy.start()
-        loads.append(copy)
 
     barrier = pltpu.get_barrier_semaphore()
     each_peer(lambda k: pl.semaphore_signal(barrier, inc=1, device_id=peer(k), device_id_type=MESH))
@@ -121,6 +122,14 @@
     col_own = lax.broadcasted_iota(jnp.int32, (rows, cols), 1)
     inner_x = jnp.where(row_own < rows - 1, wet_own * up(wet_own, 0), 0.0)
     inner_y = jnp.where(col_own < cols - 1, wet_own * up(wet_own, 1), 0.0)
+    tiles = cols // LANES
+    for f, x in enumerate((deep_own, damp_own)):
+        for c in range(tiles):
+            span = slice(c * LANES, (c + 1) * LANES)
+            send_west[f * tiles + c] = x[:HALO, span]
+            send_east[f * tiles + c] = x[:, span]
+        send_lat[0, f] = x[:, :LANES]
+        send_lat[1, f] = x[:, cols - LANES:]
     scale = 1.0 / math.sqrt(levels)
     column = []
     for copy, buf in ((loads[0], u_buf), (loads[1], v_buf)):
@@ -137,13 +146,11 @@
     last_east = jnp.broadcast_to(east_own[rows - 1:], (rows, cols))
     part_sent = jnp.where(row_own == 0, last_east, part_own)
     own = [deep_own, damp_own, part_own, east_own, north_own]
-    tiles = cols // LANES
     lane_short = lax.broadcasted_iota(jnp.int32, (rows, LANES), 1)
-    for f, (x, y) in enumerate(((deep_own, deep_own), (damp_own, damp_own), (part_own, part_sent))):
-        for c in range(tiles):
-            span = slice(c * LANES, (c + 1) * LANES)
-            send_west[f * tiles + c] = x[:HALO, span]
-            send_east[f * tiles + c] = y[:, span]
+    for c in range(tiles):
+        span = slice(c * LANES, (c + 1) * LANES)
+        send_west[2 * tiles + c] = part_own[:HALO, span]
+        send_east[2 * tiles + c] = part_sent[:, span]
     north_last = north_own[:, cols - LANES:]
     send_west[3 * tiles] = north_last[:HALO]
     send_east[3 * tiles] = north_last
@@ -160,7 +167,7 @@
     for part in (0, 1):
         send_diag_west[part] = pack((deep_own, damp_own, part_own, north_own), part)[:HALO]
         send_diag_east[part] = pack((deep_own, damp_own, part_sent, north_own), part)
-    for f in range(FIELDS):
+    for f in range(2, FIELDS):
         send_lat[0, f] = own[f][:, :LANES]
         send_lat[1, f] = own[f][:, cols - LANES:]
 

time: 15.5 us -> 15.6 us (level)
  no operation moved by 1% of the time
where the time goes in v7:
time: 15.6 us; the launch traced here: 15.3 us
  Pallas kernels  14.1 us (90%)
  between operations  0.64 us (4%)
  local copies, waits for them, and re-layouts  0.61 us (4%)
    pallas_call x1, Pallas kernels, body(): pl.pallas_call(functools.partial(kernel, lon_n, lat_n, 'lon', 'lat'), out...  14.1 us
    squeeze x1, local copies, waits for them, and re-layouts, body(): return (both[0], both[1])  0.61 us

profile of v7, /device:TPU:0, one launch (start us, length us, event | category | flops | bytes accessed | tf_op | source)
XLA Modules:
  0.0 15.3 jit_solution(14929756808678348442)
XLA Ops:
  0.6 14.1 %shard_map.86 = f32[2,8,512]{2,1,0:T(8,128)S(1)} custom-call(f32[40]{0:T(128)} %thick_hbm.1, f32[40,8,512]{2,1,0:T(8,128)} %u_hbm.1, f32[40,8,512]{2,1,0:T(8,128)} %v_hbm.1, f32[8,512]{1,0:T(8,128)} %depth_hbm.1, s32[8,512]{1,0:T(8,128)} %mask_hbm.1, f32[8,512]{1,0:T(8,128)} %damp_hbm.1, f32[8,512]{1,0:T(8,128)} %eta_hbm.1), custom_call_target="tpu_custom_call" | custom-call | tf_op jit(solution)/shard_map/pallas_call | solution.py:365
  14.7 0.6 %slice_bitcast_fusion = (f32[8,512]{1,0:T(8,128)}, f32[8,512]{1,0:T(8,128)}) fusion(f32[2,8,512]{2,1,0:T(8,128)S(1)} %shard_map.86), kind=kLoop, calls=%fused_computation | loop fusion | bytes 65536 | tf_op jit(solution)/shard_map/squeeze | solution.py:398
